TPU v7x, 128 devices: a whole 4x4x4 slice. The times are simulated.
128 devices in a mesh: section: 8 (over y, core), dp: 16 (over z, x).
Axes of the slice: x: 4, y: 4, z: 4, core: 2. Of those that a mesh axis runs over, the one named last changes fastest.
Arguments:
- acts: bfloat16 [8, 8192, 3584], P('section', 'dp'), may hold values from -400 to 400
- cotangent: bfloat16 [8192, 3584], P('dp'), may hold values from -6 to 6
- frozen: bfloat16 [8, 3584, 3584], P('section', 'dp'), may hold values from -0.09375 to 0.09375
- down_adapter: bfloat16 [8, 16, 3584], P('section'), may hold values from -0.25 to 0.25
- up_adapter: bfloat16 [8, 16, 3584], P('section'), may hold values from -0.25 to 0.25
- example_ids: int32 [16, 4], P('dp'), may hold values from 0 to 3, each once within a row
- lengths: int32 [16, 4], P('dp'), may hold values from 32 to 128
Outputs:
- grad_down: float32 [8, 16, 3584], P('section', None, 'dp')
- grad_up: float32 [8, 16, 3584], P('section', None, 'dp')
- example_norms: float32 [16, 4], P('dp')
Inputs may be any that keep to these rules, and one draw needn't show every extreme that they name: `example_ids`: each row is an ordering of the 4 examples of one replica.
All inputs are finite; a program needn't handle non-finite values.
Results may differ from a plain program's by a relative error of at most 0.009.
Values may be sent and summed in bfloat16 or wider, within the bound.
A program may use at most 128 MiB of HBM per device.

v0:
```python
import math
import jax
import jax.numpy as jnp
from jax import lax
from jax.sharding import PartitionSpec as P


def from_behind(value, axis, steps):
    count = lax.axis_size(axis)
    first, last = (max(0, -steps), min(count, count - steps))
    return lax.ppermute(value, axis, [(source, source + steps) for source in range(first, last)])


def sent_to_all(value, axis):
    size = lax.axis_size(axis)
    return lax.all_to_all(
        jnp.broadcast_to(value[None], (size, *value.shape)), axis, 0, 0, tiled=True
    )


def taken_together(value, axis):
    return sent_to_all(value, axis).sum(axis=0)


def split_up(value, dim, size):
    shape = value.shape
    pieces = value.reshape(*shape[:dim], size, shape[dim] // size, *shape[dim + 1 :])
    return jnp.moveaxis(pieces, dim, 0)


def sent_and_summed(value, axis, dim):
    pieces = split_up(value, dim, lax.axis_size(axis))
    arrived = lax.all_to_all(pieces, axis, split_axis=0, concat_axis=0, tiled=True)
    return arrived.sum(axis=0)


def side_by_side(arrays, axis, dim, along):
    ends, at = ([], 0)
    for a in arrays[:-1]:
        at += a.shape[along]
        ends.append(at)
    both = jnp.concatenate(arrays, axis=along)
    return tuple(jnp.split(sent_and_summed(both, axis, dim), ends, axis=along))


def on_device(acts, cotangent, frozen, down_adapter, up_adapter, example_ids, lengths):
    section_count = lax.axis_size("section")
    section_index = lax.axis_index("section")
    replica_count = lax.axis_size("dp")
    layer_inputs = acts[0]
    down_rows = down_adapter[0]
    up_rows = up_adapter[0]
    slot_count = example_ids.shape[1]
    positions = layer_inputs.shape[0] // slot_count
    features = layer_inputs.shape[1]
    rank_size = down_rows.shape[0]
    choose = (example_ids[0][:, None] == jnp.arange(slot_count, dtype=jnp.int32)[None, :]).astype(
        jnp.int32
    )
    slot_length = jnp.sum(choose * lengths[0][None, :], axis=1)
    live_mask = (jnp.arange(positions, dtype=jnp.int32)[None, :] < slot_length[:, None]).astype(
        jnp.bfloat16
    )
    seeded = cotangent.reshape(slot_count, positions, features) * live_mask[:, :, None]
    input_blocks = layer_inputs.reshape(slot_count, positions, features)
    clip_scale = math.sqrt(2.0 * rank_size * features) / math.sqrt(replica_count * slot_count)
    weight = lax.all_gather(frozen[0], "dp", axis=0, tiled=True)

    def backstep(out_grad):
        up_grad = jnp.dot(out_grad, up_rows.T, preferred_element_type=jnp.float32).astype(
            jnp.bfloat16
        )
        in_grad = jnp.dot(out_grad, weight.T, preferred_element_type=jnp.float32)
        in_grad = in_grad + jnp.dot(up_grad, down_rows, preferred_element_type=jnp.float32)
        return in_grad.astype(jnp.bfloat16)

    def local_terms(out_grad, inputs):
        up_grad = jnp.dot(out_grad, up_rows.T, preferred_element_type=jnp.float32).astype(
            jnp.bfloat16
        )
        down_act = jnp.dot(inputs, down_rows.T, preferred_element_type=jnp.float32).astype(
            jnp.bfloat16
        )
        down_term = jnp.dot(up_grad.T, inputs, preferred_element_type=jnp.float32)
        up_term = jnp.dot(down_act.T, out_grad, preferred_element_type=jnp.float32)
        square_sum = jnp.sum(down_term * down_term) + jnp.sum(up_term * up_term)
        return (square_sum, down_term, up_term)

    tick_count = slot_count + section_count - 1
    incoming = jnp.zeros((positions, features), jnp.bfloat16)
    stored_grads = jnp.zeros((slot_count, positions, features), jnp.bfloat16)
    sum_down = jnp.zeros((rank_size, features), jnp.float32)
    sum_up = jnp.zeros((rank_size, features), jnp.float32)
    slot_norms = jnp.zeros((slot_count,), jnp.float32)

    def tick_step(tick, carry):
        incoming, stored_grads, sum_down, sum_up, slot_norms = carry
        micro_index = tick - (section_count - 1 - section_index)
        active = (micro_index >= 0) & (micro_index < slot_count)
        held_index = jnp.clip(micro_index, 0, slot_count - 1)
        fresh = lax.dynamic_index_in_dim(seeded, held_index, 0, keepdims=False)
        start = jnp.where(section_index == section_count - 1, fresh, incoming)
        produced = lax.cond(active, backstep, lambda value: jnp.zeros_like(value), start)
        previous = lax.dynamic_index_in_dim(stored_grads, held_index, 0, keepdims=False)
        kept = jnp.where(active, start, previous)
        stored_grads = lax.dynamic_update_index_in_dim(stored_grads, kept, held_index, 0)
        incoming = from_behind(produced, "section", -1)
        return (incoming, stored_grads, sum_down, sum_up, slot_norms)

    carry = (incoming, stored_grads, sum_down, sum_up, slot_norms)
    incoming, stored_grads, sum_down, sum_up, slot_norms = lax.fori_loop(
        0, tick_count, tick_step, carry
    )
    square_sums, down_terms, up_terms = jax.vmap(local_terms)(stored_grads, input_blocks)
    totals = taken_together(square_sums, "section")
    slot_norms = jnp.sqrt(totals)
    factors = clip_scale / (slot_norms + 0.01)
    sum_down = jnp.sum(factors[:, None, None] * down_terms, axis=0)
    sum_up = jnp.sum(factors[:, None, None] * up_terms, axis=0)
    grad_down, grad_up = side_by_side((sum_down, sum_up), "dp", 1, 0)
    example_norms = jnp.sum(choose.astype(jnp.float32) * slot_norms[:, None], axis=0)
    return (grad_down[None], grad_up[None], example_norms[None])


def solution(mesh):
    in_specs = (
        P("section", "dp", None),
        P("dp", None),
        P("section", "dp", None),
        P("section", None, None),
        P("section", None, None),
        P("dp", None),
        P("dp", None),
    )
    out_specs = (P("section", None, "dp"), P("section", None, "dp"), P("dp", None))
    return jax.shard_map(
        on_device, mesh=mesh, in_specs=in_specs, out_specs=out_specs, check_vma=False
    )
```

profile of v0, /device:TPU:0, one launch (start us, length us, event | category | flops | bytes accessed | tf_op | source)
XLA Modules:
  0.0 538.0 jit_solution(118021196939126210)
XLA Ops:
  8.8 4.1 broadcast_multiply_fusion
  13.0 156.6 %all-gather.3.cloned.1.call-done = bf16[1,3584,3584]{2,1,0:T(8,128)(2,1)} async-done(((bf16[1,224,3584]{2,1,0:T(8,128)(2,1)}), bf16[1,3584,3584]{2,1,0:T(8,128)(2,1)}) %all-gather.3.cloned.1.call-update) | async-done | bytes 25690128 | tf_op jit(solution)/shard_map/all_gather | solution.py:67
  169.5 2.1 broadcast_in_dim.35
  171.7 317.0 %while.17 = (s32[]{:T(128)}, bf16[128,3584]{1,0:T(8,128)(2,1)S(1)}, bf16[4,128,3584]{2,1,0:T(8,128)(2,1)}, s32[]{:T(128)}, pred[]{:T(512)}, /*index=5*/bf16[4,12...) while((s32[]{:T(128)}, bf16[128,3584]{1,0:T(8,128)(2,1)S(1)}, ...), condition=%wide.region_4.5_spmd, body=%wide.region_1.4_spmd.sunk | while | flops 3319531520 | bytes 42435348 | solution.py:111
  171.7 1.2 constant_dynamic-slice_fusion.2
  173.0 2.6 bitcast_dynamic-update-slice_fusion.2
  176.6 1.3 collective-permute-start
  177.9 3.3 collective-permute-done
  181.2 1.2 constant_dynamic-slice_fusion.2
  182.4 2.6 bitcast_dynamic-update-slice_fusion.2
  186.1 1.3 collective-permute-start
  187.4 13.0 %collective-permute-done = bf16[128,3584]{1,0:T(8,128)(2,1)S(1)} collective-permute-done((bf16[128,3584]{1,0:T(8,128)(2,1)}, bf16[128,3584]{1,0:T(8,128)(2,1)S(1)}, u32[]{:S(2)}, u32[]{:S(2)}) %collective-permute-start) | collective-permute-done | bytes 917536 | tf_op jit(solution)/shard_map/while/body/eval_jaxpr/ppermute | solution.py:11
  200.4 1.2 constant_dynamic-slice_fusion.2
  201.6 2.6 bitcast_dynamic-update-slice_fusion.2
  205.2 1.3 collective-permute-start
  206.5 13.6 %collective-permute-done = bf16[128,3584]{1,0:T(8,128)(2,1)S(1)} collective-permute-done((bf16[128,3584]{1,0:T(8,128)(2,1)}, bf16[128,3584]{1,0:T(8,128)(2,1)S(1)}, u32[]{:S(2)}, u32[]{:S(2)}) %collective-permute-start) | collective-permute-done | bytes 917536 | tf_op jit(solution)/shard_map/while/body/eval_jaxpr/ppermute | solution.py:11
  220.2 1.2 constant_dynamic-slice_fusion.2
  221.4 2.6 bitcast_dynamic-update-slice_fusion.2
  225.0 1.3 collective-permute-start
  226.3 13.6 %collective-permute-done = bf16[128,3584]{1,0:T(8,128)(2,1)S(1)} collective-permute-done((bf16[128,3584]{1,0:T(8,128)(2,1)}, bf16[128,3584]{1,0:T(8,128)(2,1)S(1)}, u32[]{:S(2)}, u32[]{:S(2)}) %collective-permute-start) | collective-permute-done | bytes 917536 | tf_op jit(solution)/shard_map/while/body/eval_jaxpr/ppermute | solution.py:11
  239.9 1.2 constant_dynamic-slice_fusion.2
  241.2 2.6 bitcast_dynamic-update-slice_fusion.2
  244.8 1.3 collective-permute-start
  246.1 13.6 %collective-permute-done = bf16[128,3584]{1,0:T(8,128)(2,1)S(1)} collective-permute-done((bf16[128,3584]{1,0:T(8,128)(2,1)}, bf16[128,3584]{1,0:T(8,128)(2,1)S(1)}, u32[]{:S(2)}, u32[]{:S(2)}) %collective-permute-start) | collective-permute-done | bytes 917536 | tf_op jit(solution)/shard_map/while/body/eval_jaxpr/ppermute | solution.py:11
  259.7 1.2 constant_dynamic-slice_fusion.2
  261.0 2.6 bitcast_dynamic-update-slice_fusion.2
  264.6 1.3 collective-permute-start
  265.9 13.6 %collective-permute-done = bf16[128,3584]{1,0:T(8,128)(2,1)S(1)} collective-permute-done((bf16[128,3584]{1,0:T(8,128)(2,1)}, bf16[128,3584]{1,0:T(8,128)(2,1)S(1)}, u32[]{:S(2)}, u32[]{:S(2)}) %collective-permute-start) | collective-permute-done | bytes 917536 | tf_op jit(solution)/shard_map/while/body/eval_jaxpr/ppermute | solution.py:11
  279.5 1.2 constant_dynamic-slice_fusion.2
  280.8 2.6 bitcast_dynamic-update-slice_fusion.2
  284.4 1.3 collective-permute-start
  285.7 78.1 %collective-permute-done = bf16[128,3584]{1,0:T(8,128)(2,1)S(1)} collective-permute-done((bf16[128,3584]{1,0:T(8,128)(2,1)}, bf16[128,3584]{1,0:T(8,128)(2,1)S(1)}, u32[]{:S(2)}, u32[]{:S(2)}) %collective-permute-start) | collective-permute-done | bytes 917536 | tf_op jit(solution)/shard_map/while/body/eval_jaxpr/ppermute | solution.py:11
  363.8 1.2 constant_dynamic-slice_fusion.2
  365.0 2.6 bitcast_dynamic-update-slice_fusion.2
  367.6 15.1 %conditional.2 = (bf16[128,3584]{1,0:T(8,128)(2,1)}) conditional(s32[]{:T(128)} %convert_element_type.57, () %tuple.55, (bf16[128,3584]{1,0:T(8,128)(2,1)S(1)}, bf16[3584,3584]{1,0:T(8,128)(2,1)}, bf16[16,3584]{1,0:T(8,128)(2,1)S(1)}, bf16[16,3584]{1,0:T(8,128)(2,1)S(1)}) %tuple.56), branch_computations={%region_2.2_spmd, %region_3.3_spmd} | conditional | flops 3318614016 | bytes 32342024 | solution.py:103
  367.6 12.9 %fusion.13 = f32[128,3584]{1,0:T(8,128)S(1)} fusion(bf16[128,3584]{1,0:T(8,128)(2,1)S(1)} %get-tuple-element.202, bf16[3584,3584]{1,0:T(8,128)(2,1)} %get-tuple-element.203), kind=kOutput, calls=%fused_computation.28 | convolution fusion | flops 3288334336 | bytes 28442624 | tf_op jit(solution)/shard_map/while/body/eval_jaxpr/cond/branch_1_fun/dot_general | solution.py:73
  380.5 2.2 fusion
  382.7 1.3 collective-permute-start
  384.0 13.6 %collective-permute-done = bf16[128,3584]{1,0:T(8,128)(2,1)S(1)} collective-permute-done((bf16[128,3584]{1,0:T(8,128)(2,1)}, bf16[128,3584]{1,0:T(8,128)(2,1)S(1)}, u32[]{:S(2)}, u32[]{:S(2)}) %collective-permute-start) | collective-permute-done | bytes 917536 | tf_op jit(solution)/shard_map/while/body/eval_jaxpr/ppermute | solution.py:11
  397.6 1.2 constant_dynamic-slice_fusion.2
  398.8 2.6 bitcast_dynamic-update-slice_fusion.2
  401.4 15.1 %conditional.2 = (bf16[128,3584]{1,0:T(8,128)(2,1)}) conditional(s32[]{:T(128)} %convert_element_type.57, () %tuple.55, (bf16[128,3584]{1,0:T(8,128)(2,1)S(1)}, bf16[3584,3584]{1,0:T(8,128)(2,1)}, bf16[16,3584]{1,0:T(8,128)(2,1)S(1)}, bf16[16,3584]{1,0:T(8,128)(2,1)S(1)}) %tuple.56), branch_computations={%region_2.2_spmd, %region_3.3_spmd} | conditional | flops 3318614016 | bytes 32342024 | solution.py:103
  401.4 12.9 %fusion.13 = f32[128,3584]{1,0:T(8,128)S(1)} fusion(bf16[128,3584]{1,0:T(8,128)(2,1)S(1)} %get-tuple-element.202, bf16[3584,3584]{1,0:T(8,128)(2,1)} %get-tuple-element.203), kind=kOutput, calls=%fused_computation.28 | convolution fusion | flops 3288334336 | bytes 28442624 | tf_op jit(solution)/shard_map/while/body/eval_jaxpr/cond/branch_1_fun/dot_general | solution.py:73
  414.3 2.2 fusion
  416.5 1.3 collective-permute-start
  417.8 13.6 %collective-permute-done = bf16[128,3584]{1,0:T(8,128)(2,1)S(1)} collective-permute-done((bf16[128,3584]{1,0:T(8,128)(2,1)}, bf16[128,3584]{1,0:T(8,128)(2,1)S(1)}, u32[]{:S(2)}, u32[]{:S(2)}) %collective-permute-start) | collective-permute-done | bytes 917536 | tf_op jit(solution)/shard_map/while/body/eval_jaxpr/ppermute | solution.py:11
  432.6 2.6 bitcast_dynamic-update-slice_fusion.2
  435.2 15.1 %conditional.2 = (bf16[128,3584]{1,0:T(8,128)(2,1)}) conditional(s32[]{:T(128)} %convert_element_type.57, () %tuple.55, (bf16[128,3584]{1,0:T(8,128)(2,1)S(1)}, bf16[3584,3584]{1,0:T(8,128)(2,1)}, bf16[16,3584]{1,0:T(8,128)(2,1)S(1)}, bf16[16,3584]{1,0:T(8,128)(2,1)S(1)}) %tuple.56), branch_computations={%region_2.2_spmd, %region_3.3_spmd} | conditional | flops 3318614016 | bytes 32342024 | solution.py:103
  435.2 12.9 %fusion.13 = f32[128,3584]{1,0:T(8,128)S(1)} fusion(bf16[128,3584]{1,0:T(8,128)(2,1)S(1)} %get-tuple-element.202, bf16[3584,3584]{1,0:T(8,128)(2,1)} %get-tuple-element.203), kind=kOutput, calls=%fused_computation.28 | convolution fusion | flops 3288334336 | bytes 28442624 | tf_op jit(solution)/shard_map/while/body/eval_jaxpr/cond/branch_1_fun/dot_general | solution.py:73
  448.1 2.2 fusion
  450.3 1.3 collective-permute-start
  451.6 13.6 %collective-permute-done = bf16[128,3584]{1,0:T(8,128)(2,1)S(1)} collective-permute-done((bf16[128,3584]{1,0:T(8,128)(2,1)}, bf16[128,3584]{1,0:T(8,128)(2,1)S(1)}, u32[]{:S(2)}, u32[]{:S(2)}) %collective-permute-start) | collective-permute-done | bytes 917536 | tf_op jit(solution)/shard_map/while/body/eval_jaxpr/ppermute | solution.py:11
  465.2 1.2 constant_dynamic-slice_fusion.2
  466.4 2.6 bitcast_dynamic-update-slice_fusion.2
  469.0 15.1 %conditional.2 = (bf16[128,3584]{1,0:T(8,128)(2,1)}) conditional(s32[]{:T(128)} %convert_element_type.57, () %tuple.55, (bf16[128,3584]{1,0:T(8,128)(2,1)S(1)}, bf16[3584,3584]{1,0:T(8,128)(2,1)}, bf16[16,3584]{1,0:T(8,128)(2,1)S(1)}, bf16[16,3584]{1,0:T(8,128)(2,1)S(1)}) %tuple.56), branch_computations={%region_2.2_spmd, %region_3.3_spmd} | conditional | flops 3318614016 | bytes 32342024 | solution.py:103
  469.0 12.9 %fusion.13 = f32[128,3584]{1,0:T(8,128)S(1)} fusion(bf16[128,3584]{1,0:T(8,128)(2,1)S(1)} %get-tuple-element.202, bf16[3584,3584]{1,0:T(8,128)(2,1)} %get-tuple-element.203), kind=kOutput, calls=%fused_computation.28 | convolution fusion | flops 3288334336 | bytes 28442624 | tf_op jit(solution)/shard_map/while/body/eval_jaxpr/cond/branch_1_fun/dot_general | solution.py:73
  481.9 2.2 fusion
  484.1 1.3 collective-permute-start
  485.4 3.3 collective-permute-done
  488.7 4.9 multiply_reduce_fusion.3
  493.6 4.9 multiply_reduce_fusion.2
  498.5 13.5 %all_to_all.11 = f32[8,1,4]{2,1,0:T(1,128)S(1)} all-to-all(f32[8,1,4]{2,1,0:T(1,128)S(1)} %broadcast_in_dim.36), channel_id=1, replica_groups=mesh['section'=8,'dp'=16] {'section'}, dimensions={0} | all-to-all | bytes 256 | tf_op jit(solution)/shard_map/all_to_all | solution.py:16
  513.7 5.3 all-to-all-start.1
  519.6 10.9 %all-to-all-done.1 = f32[16,32,224]{2,1,0:T(8,128)S(1)} async-done(((f32[16,32,224]{2,1,0:T(8,128)}), f32[16,32,224]{2,1,0:T(8,128)S(1)}, u32[]{:S(2)}, u32[]{:S(2)}) %all-to-all-start.1) | async-done | bytes 458784 | tf_op jit(solution)/shard_map/all_to_all | solution.py:33
  (37 shorter events, 20.2 us)
Async XLA Ops:
  7.2 162.4 %all-gather.3.cloned.1.call-start = ((), (), s32[]{:S(2)}) async-start(), calls=%async_computation.2 | async-start | bytes 27295744 | tf_op jit(solution)/shard_map/all_gather | solution.py:67
  13.0 158.7 %copy-start = (bf16[1,16,3584]{2,1,0:T(8,128)(2,1)S(1)}, bf16[1,16,3584]{2,1,0:T(8,128)(2,1)}, u32[]{:S(2)}) copy-start(bf16[1,16,3584]{2,1,0:T(8,128)(2,1)} %param.15) | copy-start | bytes 344068
  13.0 158.7 %copy-start.1 = (bf16[1,16,3584]{2,1,0:T(8,128)(2,1)S(1)}, bf16[1,16,3584]{2,1,0:T(8,128)(2,1)}, u32[]{:S(2)}) copy-start(bf16[1,16,3584]{2,1,0:T(8,128)(2,1)} %param.14) | copy-start | bytes 344068
  176.6 4.6 collective-permute-start
  186.1 14.3 %collective-permute-start = (bf16[128,3584]{1,0:T(8,128)(2,1)}, bf16[128,3584]{1,0:T(8,128)(2,1)S(1)}, u32[]{:S(2)}, u32[]{:S(2)}) collective-permute-start(bf16[128,3584]{1,0:T(8,128)(2,1)} %get-tuple-element.349), channel_id=1, source_target_pairs={{16,0},{32,16},{48,32},{64,48},{80,64},{96,80},{112,96},{17,1},{33... | collective-permute-start | bytes 2752520 | tf_op jit(solution)/shard_map/while/body/eval_jaxpr/ppermute | solution.py:11
  205.2 14.9 %collective-permute-start = (bf16[128,3584]{1,0:T(8,128)(2,1)}, bf16[128,3584]{1,0:T(8,128)(2,1)S(1)}, u32[]{:S(2)}, u32[]{:S(2)}) collective-permute-start(bf16[128,3584]{1,0:T(8,128)(2,1)} %get-tuple-element.349), channel_id=1, source_target_pairs={{16,0},{32,16},{48,32},{64,48},{80,64},{96,80},{112,96},{17,1},{33... | collective-permute-start | bytes 2752520 | tf_op jit(solution)/shard_map/while/body/eval_jaxpr/ppermute | solution.py:11
  225.0 14.9 %collective-permute-start = (bf16[128,3584]{1,0:T(8,128)(2,1)}, bf16[128,3584]{1,0:T(8,128)(2,1)S(1)}, u32[]{:S(2)}, u32[]{:S(2)}) collective-permute-start(bf16[128,3584]{1,0:T(8,128)(2,1)} %get-tuple-element.349), channel_id=1, source_target_pairs={{16,0},{32,16},{48,32},{64,48},{80,64},{96,80},{112,96},{17,1},{33... | collective-permute-start | bytes 2752520 | tf_op jit(solution)/shard_map/while/body/eval_jaxpr/ppermute | solution.py:11
  244.8 14.9 %collective-permute-start = (bf16[128,3584]{1,0:T(8,128)(2,1)}, bf16[128,3584]{1,0:T(8,128)(2,1)S(1)}, u32[]{:S(2)}, u32[]{:S(2)}) collective-permute-start(bf16[128,3584]{1,0:T(8,128)(2,1)} %get-tuple-element.349), channel_id=1, source_target_pairs={{16,0},{32,16},{48,32},{64,48},{80,64},{96,80},{112,96},{17,1},{33... | collective-permute-start | bytes 2752520 | tf_op jit(solution)/shard_map/while/body/eval_jaxpr/ppermute | solution.py:11
  264.6 14.9 %collective-permute-start = (bf16[128,3584]{1,0:T(8,128)(2,1)}, bf16[128,3584]{1,0:T(8,128)(2,1)S(1)}, u32[]{:S(2)}, u32[]{:S(2)}) collective-permute-start(bf16[128,3584]{1,0:T(8,128)(2,1)} %get-tuple-element.349), channel_id=1, source_target_pairs={{16,0},{32,16},{48,32},{64,48},{80,64},{96,80},{112,96},{17,1},{33... | collective-permute-start | bytes 2752520 | tf_op jit(solution)/shard_map/while/body/eval_jaxpr/ppermute | solution.py:11
  284.4 79.4 %collective-permute-start = (bf16[128,3584]{1,0:T(8,128)(2,1)}, bf16[128,3584]{1,0:T(8,128)(2,1)S(1)}, u32[]{:S(2)}, u32[]{:S(2)}) collective-permute-start(bf16[128,3584]{1,0:T(8,128)(2,1)} %get-tuple-element.349), channel_id=1, source_target_pairs={{16,0},{32,16},{48,32},{64,48},{80,64},{96,80},{112,96},{17,1},{33... | collective-permute-start | bytes 2752520 | tf_op jit(solution)/shard_map/while/body/eval_jaxpr/ppermute | solution.py:11
  382.7 14.9 %collective-permute-start = (bf16[128,3584]{1,0:T(8,128)(2,1)}, bf16[128,3584]{1,0:T(8,128)(2,1)S(1)}, u32[]{:S(2)}, u32[]{:S(2)}) collective-permute-start(bf16[128,3584]{1,0:T(8,128)(2,1)} %get-tuple-element.349), channel_id=1, source_target_pairs={{16,0},{32,16},{48,32},{64,48},{80,64},{96,80},{112,96},{17,1},{33... | collective-permute-start | bytes 2752520 | tf_op jit(solution)/shard_map/while/body/eval_jaxpr/ppermute | solution.py:11
  416.5 14.9 %collective-permute-start = (bf16[128,3584]{1,0:T(8,128)(2,1)}, bf16[128,3584]{1,0:T(8,128)(2,1)S(1)}, u32[]{:S(2)}, u32[]{:S(2)}) collective-permute-start(bf16[128,3584]{1,0:T(8,128)(2,1)} %get-tuple-element.349), channel_id=1, source_target_pairs={{16,0},{32,16},{48,32},{64,48},{80,64},{96,80},{112,96},{17,1},{33... | collective-permute-start | bytes 2752520 | tf_op jit(solution)/shard_map/while/body/eval_jaxpr/ppermute | solution.py:11
  450.3 14.9 %collective-permute-start = (bf16[128,3584]{1,0:T(8,128)(2,1)}, bf16[128,3584]{1,0:T(8,128)(2,1)S(1)}, u32[]{:S(2)}, u32[]{:S(2)}) collective-permute-start(bf16[128,3584]{1,0:T(8,128)(2,1)} %get-tuple-element.349), channel_id=1, source_target_pairs={{16,0},{32,16},{48,32},{64,48},{80,64},{96,80},{112,96},{17,1},{33... | collective-permute-start | bytes 2752520 | tf_op jit(solution)/shard_map/while/body/eval_jaxpr/ppermute | solution.py:11
  484.1 4.6 collective-permute-start
  498.4 20.5 %copy-start.2 = (s32[1,4]{1,0:T(1,128)S(1)}, s32[1,4]{1,0:T(1,128)}, u32[]{:S(2)}) copy-start(s32[1,4]{1,0:T(1,128)} %param.16) | copy-start | bytes 52
  513.7 16.8 %all-to-all-start.1 = ((f32[16,32,224]{2,1,0:T(8,128)}), f32[16,32,224]{2,1,0:T(8,128)S(1)}, u32[]{:S(2)}, u32[]{:S(2)}) async-start(f32[16,32,224]{2,1,0:T(8,128)} %copy.13), calls=%async_computation.1 | async-start | bytes 1048576 | tf_op jit(solution)/shard_map/all_to_all | solution.py:33
Sparse Core Ops, SparseCore 0:
  10.1 159.3 all-gather.2
where the time goes:
time: 539 us; the launch traced here: 538 us
  waiting for transfers between devices  361 us (67%)
  matrix products  70.1 us (13%)
  other arithmetic  34.6 us (6%)
  local copies, waits for them, and re-layouts  25 us (5%)
  starting transfers between devices  19.4 us (4%)
  between operations  14.1 us (3%)
  blocking collectives  13.5 us (3%)
    ppermute x11, waiting for transfers between devices, from_behind(): lax.ppermute(value, axis, [(source, source + steps) for source in range(f...  193 us
    all_gather x1, waiting for transfers between devices, on_device(): weight = lax.all_gather(frozen[0], 'dp', axis=0, tiled=True)  157 us
    dot_general x4, matrix products, backstep(): in_grad = jnp.dot(out_grad, weight.T, preferred_element_type=jnp.float32)  51.6 us
    dynamic_update_slice x11, other arithmetic, tick_step(): lax.dynamic_update_index_in_dim(stored_grads, kept, held_index, 0)  28.6 us
    ppermute x11, starting transfers between devices, from_behind(): lax.ppermute(value, axis, [(source, source + steps) for source in range(f...  14.1 us
    dynamic_slice x11, local copies, waits for them, and re-layouts, tick_step(): lax.dynamic_index_in_dim(stored_grads, held_index, 0, keepdims=False)  13.6 us
    all_to_all x1, blocking collectives, sent_to_all(): lax.all_to_all(jnp.broadcast_to(value[None], (size, *value.shape)), axis,...  13.5 us
    all_to_all x1, waiting for transfers between devices, sent_and_summed(): lax.all_to_all(pieces, axis, split_axis=0, concat_axis=0, tiled=True)  10.9 us
  transfers between devices with their start and end apart: 13, of which 13 were waited for; matrix products, arithmetic and copies ran while one was open for 1% of the time, Pallas kernels for 0%

commit v1 on v0

--- a/solution.py
+++ b/solution.py
@@ -64,7 +64,9 @@
     seeded = cotangent.reshape(slot_count, positions, features) * live_mask[:, :, None]
     input_blocks = layer_inputs.reshape(slot_count, positions, features)
     clip_scale = math.sqrt(2.0 * rank_size * features) / math.sqrt(replica_count * slot_count)
-    weight = lax.all_gather(frozen[0], "dp", axis=0, tiled=True)
+    weight = jnp.concatenate(
+        lax.all_to_all(jnp.stack([frozen[0]] * lax.axis_size("dp")), "dp", 0, 0), axis=0
+    )
 
     def backstep(out_grad):
         up_grad = jnp.dot(out_grad, up_rows.T, preferred_element_type=jnp.float32).astype(

time: 539 us -> 764 us (1.42)
  waiting for transfers between devices: 361 us -> 583 us
  between operations: 14.1 us -> 0.73 us
  local copies, waits for them, and re-layouts: 25 us -> 34.8 us
    all_to_all x0 -> x1, waiting for transfers between devices: none -> 379 us  [on_device(): lax.all_to_all(jnp.stack([frozen[0]] * lax.axis_size('dp')), 'dp', 0, 0)]
    all_gather x1 -> x0, waiting for transfers between devices: 157 us -> none  [on_device(): weight = lax.all_gather(frozen[0], 'dp', axis=0, tiled=True)]
    another operation x8 -> x9, local copies, waits for them, and re-layouts: 7.19 us -> 17 us  [the longest x1 9.6 us: on_device(): jnp.stack([frozen[0]] * lax.axis_size('dp'))]
    all_to_all x0 -> x1, starting transfers between devices: none -> 8.18 us  [on_device(): lax.all_to_all(jnp.stack([frozen[0]] * lax.axis_size('dp')), 'dp', 0, 0)]
where the time goes in v1:
time: 764 us; the launch traced here: 762 us
  waiting for transfers between devices  583 us (76%)
  matrix products  70.2 us (9%)
  local copies, waits for them, and re-layouts  34.8 us (5%)
  other arithmetic  34.1 us (4%)
  starting transfers between devices  25.8 us (3%)
  blocking collectives  13.5 us (2%)
    all_to_all x1, waiting for transfers between devices, on_device(): lax.all_to_all(jnp.stack([frozen[0]] * lax.axis_size('dp')), 'dp', 0, 0)  379 us
    ppermute x11, waiting for transfers between devices, from_behind(): lax.ppermute(value, axis, [(source, source + steps) for source in range(f...  192 us
    dot_general x4, matrix products, backstep(): in_grad = jnp.dot(out_grad, weight.T, preferred_element_type=jnp.float32)  51.6 us
    dynamic_update_slice x11, other arithmetic, tick_step(): lax.dynamic_update_index_in_dim(stored_grads, kept, held_index, 0)  28.7 us
  transfers between devices with their start and end apart: 13, of which 13 were waited for; matrix products, arithmetic and copies ran while one was open for 1% of the time, Pallas kernels for 0%

profile of v1, /device:TPU:0, one launch (start us, length us, event | category | flops | bytes accessed | tf_op | source)
XLA Modules:
  0.0 762.1 jit_solution(15620111590895417232)
XLA Ops:
  0.6 9.6 %stack.3 = bf16[16,224,3584]{2,1,0:T(8,128)(2,1)} broadcast(bf16[224,3584]{1,0:T(8,128)(2,1)} %bitcast.56), dimensions={1,2} | broadcast | bytes 27295744 | tf_op jit(solution)/shard_map/stack | solution.py:68
  10.2 8.2 %all-to-all-start = ((bf16[16,224,3584]{2,1,0:T(8,128)(2,1)}), bf16[16,224,3584]{2,1,0:T(8,128)(2,1)}, u32[]{:S(2)}, u32[]{:S(2)}) async-start(bf16[16,224,3584]{2,1,0:T(8,128)(2,1)} %stack.3), calls=%async_computation | async-start | bytes 51380224 | tf_op jit(solution)/shard_map/all_to_all | solution.py:68
  18.7 4.2 broadcast_multiply_fusion
  23.0 379.3 %all-to-all-done = bf16[16,224,3584]{2,1,0:T(8,128)(2,1)} async-done(((bf16[16,224,3584]{2,1,0:T(8,128)(2,1)}), bf16[16,224,3584]{2,1,0:T(8,128)(2,1)}, u32[]{:S(2)}, u32[]{:S(2)}) %all-to-all-start) | async-done | bytes 25690144 | tf_op jit(solution)/shard_map/all_to_all | solution.py:68
  402.3 2.1 broadcast_in_dim.35
  404.4 316.7 %while.17 = (s32[]{:T(128)}, bf16[128,3584]{1,0:T(8,128)(2,1)S(1)}, bf16[4,128,3584]{2,1,0:T(8,128)(2,1)}, s32[]{:T(128)}, pred[]{:T(512)}, /*index=5*/bf16[4,12...) while((s32[]{:T(128)}, bf16[128,3584]{1,0:T(8,128)(2,1)S(1)}, ...), condition=%wide.region_4.5_spmd, body=%wide.region_1.4_spmd.sunk | while | flops 3319531520 | bytes 42435348 | solution.py:113
  404.4 1.2 constant_dynamic-slice_fusion.2
  405.7 2.6 bitcast_dynamic-update-slice_fusion.2
  409.4 1.3 collective-permute-start
  410.7 3.3 collective-permute-done
  413.9 1.2 constant_dynamic-slice_fusion.2
  415.2 2.6 bitcast_dynamic-update-slice_fusion.2
  418.8 1.3 collective-permute-start
  420.1 13.1 %collective-permute-done = bf16[128,3584]{1,0:T(8,128)(2,1)S(1)} collective-permute-done((bf16[128,3584]{1,0:T(8,128)(2,1)}, bf16[128,3584]{1,0:T(8,128)(2,1)S(1)}, u32[]{:S(2)}, u32[]{:S(2)}) %collective-permute-start) | collective-permute-done | bytes 917536 | tf_op jit(solution)/shard_map/while/body/eval_jaxpr/ppermute | solution.py:11
  433.2 1.2 constant_dynamic-slice_fusion.2
  434.5 2.6 bitcast_dynamic-update-slice_fusion.2
  438.1 1.3 collective-permute-start
  439.4 13.6 %collective-permute-done = bf16[128,3584]{1,0:T(8,128)(2,1)S(1)} collective-permute-done((bf16[128,3584]{1,0:T(8,128)(2,1)}, bf16[128,3584]{1,0:T(8,128)(2,1)S(1)}, u32[]{:S(2)}, u32[]{:S(2)}) %collective-permute-start) | collective-permute-done | bytes 917536 | tf_op jit(solution)/shard_map/while/body/eval_jaxpr/ppermute | solution.py:11
  453.1 1.2 constant_dynamic-slice_fusion.2
  454.3 2.6 bitcast_dynamic-update-slice_fusion.2
  458.0 1.3 collective-permute-start
  459.3 13.6 %collective-permute-done = bf16[128,3584]{1,0:T(8,128)(2,1)S(1)} collective-permute-done((bf16[128,3584]{1,0:T(8,128)(2,1)}, bf16[128,3584]{1,0:T(8,128)(2,1)S(1)}, u32[]{:S(2)}, u32[]{:S(2)}) %collective-permute-start) | collective-permute-done | bytes 917536 | tf_op jit(solution)/shard_map/while/body/eval_jaxpr/ppermute | solution.py:11
  472.9 1.2 constant_dynamic-slice_fusion.2
  474.1 2.6 bitcast_dynamic-update-slice_fusion.2
  477.8 1.3 collective-permute-start
  479.1 13.6 %collective-permute-done = bf16[128,3584]{1,0:T(8,128)(2,1)S(1)} collective-permute-done((bf16[128,3584]{1,0:T(8,128)(2,1)}, bf16[128,3584]{1,0:T(8,128)(2,1)S(1)}, u32[]{:S(2)}, u32[]{:S(2)}) %collective-permute-start) | collective-permute-done | bytes 917536 | tf_op jit(solution)/shard_map/while/body/eval_jaxpr/ppermute | solution.py:11
  492.7 1.2 constant_dynamic-slice_fusion.2
  494.0 2.6 bitcast_dynamic-update-slice_fusion.2
  497.6 1.3 collective-permute-start
  498.9 13.6 %collective-permute-done = bf16[128,3584]{1,0:T(8,128)(2,1)S(1)} collective-permute-done((bf16[128,3584]{1,0:T(8,128)(2,1)}, bf16[128,3584]{1,0:T(8,128)(2,1)S(1)}, u32[]{:S(2)}, u32[]{:S(2)}) %collective-permute-start) | collective-permute-done | bytes 917536 | tf_op jit(solution)/shard_map/while/body/eval_jaxpr/ppermute | solution.py:11
  512.5 1.2 constant_dynamic-slice_fusion.2
  513.8 2.6 bitcast_dynamic-update-slice_fusion.2
  517.5 1.3 collective-permute-start
  518.8 77.3 %collective-permute-done = bf16[128,3584]{1,0:T(8,128)(2,1)S(1)} collective-permute-done((bf16[128,3584]{1,0:T(8,128)(2,1)}, bf16[128,3584]{1,0:T(8,128)(2,1)S(1)}, u32[]{:S(2)}, u32[]{:S(2)}) %collective-permute-start) | collective-permute-done | bytes 917536 | tf_op jit(solution)/shard_map/while/body/eval_jaxpr/ppermute | solution.py:11
  596.1 1.2 constant_dynamic-slice_fusion.2
  597.3 2.6 bitcast_dynamic-update-slice_fusion.2
  599.9 15.1 %conditional.2 = (bf16[128,3584]{1,0:T(8,128)(2,1)}) conditional(s32[]{:T(128)} %convert_element_type.57, () %tuple.55, (bf16[128,3584]{1,0:T(8,128)(2,1)S(1)}, bf16[3584,3584]{1,0:T(8,128)(2,1)}, bf16[16,3584]{1,0:T(8,128)(2,1)S(1)}, bf16[16,3584]{1,0:T(8,128)(2,1)S(1)}) %tuple.56), branch_computations={%region_2.2_spmd, %region_3.3_spmd} | conditional | flops 3318614016 | bytes 32342024 | solution.py:105
  599.9 12.9 %fusion.13 = f32[128,3584]{1,0:T(8,128)S(1)} fusion(bf16[128,3584]{1,0:T(8,128)(2,1)S(1)} %get-tuple-element.202, bf16[3584,3584]{1,0:T(8,128)(2,1)} %get-tuple-element.203), kind=kOutput, calls=%fused_computation.28 | convolution fusion | flops 3288334336 | bytes 28442624 | tf_op jit(solution)/shard_map/while/body/eval_jaxpr/cond/branch_1_fun/dot_general | solution.py:75
  612.8 2.2 fusion
  615.1 1.3 collective-permute-start
  616.4 13.6 %collective-permute-done = bf16[128,3584]{1,0:T(8,128)(2,1)S(1)} collective-permute-done((bf16[128,3584]{1,0:T(8,128)(2,1)}, bf16[128,3584]{1,0:T(8,128)(2,1)S(1)}, u32[]{:S(2)}, u32[]{:S(2)}) %collective-permute-start) | collective-permute-done | bytes 917536 | tf_op jit(solution)/shard_map/while/body/eval_jaxpr/ppermute | solution.py:11
  631.1 2.6 bitcast_dynamic-update-slice_fusion.2
  633.7 15.1 %conditional.2 = (bf16[128,3584]{1,0:T(8,128)(2,1)}) conditional(s32[]{:T(128)} %convert_element_type.57, () %tuple.55, (bf16[128,3584]{1,0:T(8,128)(2,1)S(1)}, bf16[3584,3584]{1,0:T(8,128)(2,1)}, bf16[16,3584]{1,0:T(8,128)(2,1)S(1)}, bf16[16,3584]{1,0:T(8,128)(2,1)S(1)}) %tuple.56), branch_computations={%region_2.2_spmd, %region_3.3_spmd} | conditional | flops 3318614016 | bytes 32342024 | solution.py:105
  633.7 12.9 %fusion.13 = f32[128,3584]{1,0:T(8,128)S(1)} fusion(bf16[128,3584]{1,0:T(8,128)(2,1)S(1)} %get-tuple-element.202, bf16[3584,3584]{1,0:T(8,128)(2,1)} %get-tuple-element.203), kind=kOutput, calls=%fused_computation.28 | convolution fusion | flops 3288334336 | bytes 28442624 | tf_op jit(solution)/shard_map/while/body/eval_jaxpr/cond/branch_1_fun/dot_general | solution.py:75
  646.6 2.2 fusion
  648.8 1.3 collective-permute-start
  650.1 13.6 %collective-permute-done = bf16[128,3584]{1,0:T(8,128)(2,1)S(1)} collective-permute-done((bf16[128,3584]{1,0:T(8,128)(2,1)}, bf16[128,3584]{1,0:T(8,128)(2,1)S(1)}, u32[]{:S(2)}, u32[]{:S(2)}) %collective-permute-start) | collective-permute-done | bytes 917536 | tf_op jit(solution)/shard_map/while/body/eval_jaxpr/ppermute | solution.py:11
  665.0 2.6 bitcast_dynamic-update-slice_fusion.2
  667.6 15.1 %conditional.2 = (bf16[128,3584]{1,0:T(8,128)(2,1)}) conditional(s32[]{:T(128)} %convert_element_type.57, () %tuple.55, (bf16[128,3584]{1,0:T(8,128)(2,1)S(1)}, bf16[3584,3584]{1,0:T(8,128)(2,1)}, bf16[16,3584]{1,0:T(8,128)(2,1)S(1)}, bf16[16,3584]{1,0:T(8,128)(2,1)S(1)}) %tuple.56), branch_computations={%region_2.2_spmd, %region_3.3_spmd} | conditional | flops 3318614016 | bytes 32342024 | solution.py:105
  667.6 12.9 %fusion.13 = f32[128,3584]{1,0:T(8,128)S(1)} fusion(bf16[128,3584]{1,0:T(8,128)(2,1)S(1)} %get-tuple-element.202, bf16[3584,3584]{1,0:T(8,128)(2,1)} %get-tuple-element.203), kind=kOutput, calls=%fused_computation.28 | convolution fusion | flops 3288334336 | bytes 28442624 | tf_op jit(solution)/shard_map/while/body/eval_jaxpr/cond/branch_1_fun/dot_general | solution.py:75
  680.5 2.2 fusion
  682.7 1.3 collective-permute-start
  684.0 13.6 %collective-permute-done = bf16[128,3584]{1,0:T(8,128)(2,1)S(1)} collective-permute-done((bf16[128,3584]{1,0:T(8,128)(2,1)}, bf16[128,3584]{1,0:T(8,128)(2,1)S(1)}, u32[]{:S(2)}, u32[]{:S(2)}) %collective-permute-start) | collective-permute-done | bytes 917536 | tf_op jit(solution)/shard_map/while/body/eval_jaxpr/ppermute | solution.py:11
  698.8 2.6 bitcast_dynamic-update-slice_fusion.2
  701.4 15.1 %conditional.2 = (bf16[128,3584]{1,0:T(8,128)(2,1)}) conditional(s32[]{:T(128)} %convert_element_type.57, () %tuple.55, (bf16[128,3584]{1,0:T(8,128)(2,1)S(1)}, bf16[3584,3584]{1,0:T(8,128)(2,1)}, bf16[16,3584]{1,0:T(8,128)(2,1)S(1)}, bf16[16,3584]{1,0:T(8,128)(2,1)S(1)}) %tuple.56), branch_computations={%region_2.2_spmd, %region_3.3_spmd} | conditional | flops 3318614016 | bytes 32342024 | solution.py:105
  701.4 12.9 %fusion.13 = f32[128,3584]{1,0:T(8,128)S(1)} fusion(bf16[128,3584]{1,0:T(8,128)(2,1)S(1)} %get-tuple-element.202, bf16[3584,3584]{1,0:T(8,128)(2,1)} %get-tuple-element.203), kind=kOutput, calls=%fused_computation.28 | convolution fusion | flops 3288334336 | bytes 28442624 | tf_op jit(solution)/shard_map/while/body/eval_jaxpr/cond/branch_1_fun/dot_general | solution.py:75
  714.3 2.2 fusion
  716.5 1.3 collective-permute-start
  717.8 3.3 collective-permute-done
  721.1 4.9 multiply_reduce_fusion.3
  726.0 4.9 multiply_reduce_fusion.2
  730.9 13.5 %all_to_all.16 = f32[8,1,4]{2,1,0:T(1,128)S(1)} all-to-all(f32[8,1,4]{2,1,0:T(1,128)S(1)} %broadcast_in_dim.36), channel_id=1, replica_groups=mesh['section'=8,'dp'=16] {'section'}, dimensions={0} | all-to-all | bytes 256 | tf_op jit(solution)/shard_map/all_to_all | solution.py:16
  746.1 3.6 all-to-all-start.2
  750.3 11.2 %all-to-all-done.2 = f32[16,32,224]{2,1,0:T(8,128)S(1)} async-done(((f32[16,32,224]{2,1,0:T(8,128)}), f32[16,32,224]{2,1,0:T(8,128)S(1)}, u32[]{:S(2)}, u32[]{:S(2)}) %all-to-all-start.2) | async-done | bytes 458784 | tf_op jit(solution)/shard_map/all_to_all | solution.py:33
  (39 shorter events, 21.8 us)
Async XLA Ops:
  10.2 8.2 %copy-start.2 = (s32[1,4]{1,0:T(1,128)S(1)}, s32[1,4]{1,0:T(1,128)}, u32[]{:S(2)}) copy-start(s32[1,4]{1,0:T(1,128)} %param.17) | copy-start | bytes 52
  10.2 8.2 %copy-start.3 = (s32[1,4]{1,0:T(1,128)S(1)}, s32[1,4]{1,0:T(1,128)}, u32[]{:S(2)}) copy-start(s32[1,4]{1,0:T(1,128)} %param.16) | copy-start | bytes 52
  10.2 392.0 %all-to-all-start = ((bf16[16,224,3584]{2,1,0:T(8,128)(2,1)}), bf16[16,224,3584]{2,1,0:T(8,128)(2,1)}, u32[]{:S(2)}, u32[]{:S(2)}) async-start(bf16[16,224,3584]{2,1,0:T(8,128)(2,1)} %stack.3), calls=%async_computation | async-start | bytes 51380224 | tf_op jit(solution)/shard_map/all_to_all | solution.py:68
  23.0 381.4 %copy-start = (bf16[1,16,3584]{2,1,0:T(8,128)(2,1)S(1)}, bf16[1,16,3584]{2,1,0:T(8,128)(2,1)}, u32[]{:S(2)}) copy-start(bf16[1,16,3584]{2,1,0:T(8,128)(2,1)} %param.15) | copy-start | bytes 344068
  23.0 381.4 %copy-start.1 = (bf16[1,16,3584]{2,1,0:T(8,128)(2,1)S(1)}, bf16[1,16,3584]{2,1,0:T(8,128)(2,1)}, u32[]{:S(2)}) copy-start(bf16[1,16,3584]{2,1,0:T(8,128)(2,1)} %param.14) | copy-start | bytes 344068
  409.4 4.6 collective-permute-start
  418.8 14.4 %collective-permute-start = (bf16[128,3584]{1,0:T(8,128)(2,1)}, bf16[128,3584]{1,0:T(8,128)(2,1)S(1)}, u32[]{:S(2)}, u32[]{:S(2)}) collective-permute-start(bf16[128,3584]{1,0:T(8,128)(2,1)} %get-tuple-element.349), channel_id=1, source_target_pairs={{16,0},{32,16},{48,32},{64,48},{80,64},{96,80},{112,96},{17,1},{33... | collective-permute-start | bytes 2752520 | tf_op jit(solution)/shard_map/while/body/eval_jaxpr/ppermute | solution.py:11
  438.1 14.9 %collective-permute-start = (bf16[128,3584]{1,0:T(8,128)(2,1)}, bf16[128,3584]{1,0:T(8,128)(2,1)S(1)}, u32[]{:S(2)}, u32[]{:S(2)}) collective-permute-start(bf16[128,3584]{1,0:T(8,128)(2,1)} %get-tuple-element.349), channel_id=1, source_target_pairs={{16,0},{32,16},{48,32},{64,48},{80,64},{96,80},{112,96},{17,1},{33... | collective-permute-start | bytes 2752520 | tf_op jit(solution)/shard_map/while/body/eval_jaxpr/ppermute | solution.py:11
  458.0 14.9 %collective-permute-start = (bf16[128,3584]{1,0:T(8,128)(2,1)}, bf16[128,3584]{1,0:T(8,128)(2,1)S(1)}, u32[]{:S(2)}, u32[]{:S(2)}) collective-permute-start(bf16[128,3584]{1,0:T(8,128)(2,1)} %get-tuple-element.349), channel_id=1, source_target_pairs={{16,0},{32,16},{48,32},{64,48},{80,64},{96,80},{112,96},{17,1},{33... | collective-permute-start | bytes 2752520 | tf_op jit(solution)/shard_map/while/body/eval_jaxpr/ppermute | solution.py:11
  477.8 14.9 %collective-permute-start = (bf16[128,3584]{1,0:T(8,128)(2,1)}, bf16[128,3584]{1,0:T(8,128)(2,1)S(1)}, u32[]{:S(2)}, u32[]{:S(2)}) collective-permute-start(bf16[128,3584]{1,0:T(8,128)(2,1)} %get-tuple-element.349), channel_id=1, source_target_pairs={{16,0},{32,16},{48,32},{64,48},{80,64},{96,80},{112,96},{17,1},{33... | collective-permute-start | bytes 2752520 | tf_op jit(solution)/shard_map/while/body/eval_jaxpr/ppermute | solution.py:11
  497.6 14.9 %collective-permute-start = (bf16[128,3584]{1,0:T(8,128)(2,1)}, bf16[128,3584]{1,0:T(8,128)(2,1)S(1)}, u32[]{:S(2)}, u32[]{:S(2)}) collective-permute-start(bf16[128,3584]{1,0:T(8,128)(2,1)} %get-tuple-element.349), channel_id=1, source_target_pairs={{16,0},{32,16},{48,32},{64,48},{80,64},{96,80},{112,96},{17,1},{33... | collective-permute-start | bytes 2752520 | tf_op jit(solution)/shard_map/while/body/eval_jaxpr/ppermute | solution.py:11
  517.5 78.6 %collective-permute-start = (bf16[128,3584]{1,0:T(8,128)(2,1)}, bf16[128,3584]{1,0:T(8,128)(2,1)S(1)}, u32[]{:S(2)}, u32[]{:S(2)}) collective-permute-start(bf16[128,3584]{1,0:T(8,128)(2,1)} %get-tuple-element.349), channel_id=1, source_target_pairs={{16,0},{32,16},{48,32},{64,48},{80,64},{96,80},{112,96},{17,1},{33... | collective-permute-start | bytes 2752520 | tf_op jit(solution)/shard_map/while/body/eval_jaxpr/ppermute | solution.py:11
  615.1 14.8 %collective-permute-start = (bf16[128,3584]{1,0:T(8,128)(2,1)}, bf16[128,3584]{1,0:T(8,128)(2,1)S(1)}, u32[]{:S(2)}, u32[]{:S(2)}) collective-permute-start(bf16[128,3584]{1,0:T(8,128)(2,1)} %get-tuple-element.349), channel_id=1, source_target_pairs={{16,0},{32,16},{48,32},{64,48},{80,64},{96,80},{112,96},{17,1},{33... | collective-permute-start | bytes 2752520 | tf_op jit(solution)/shard_map/while/body/eval_jaxpr/ppermute | solution.py:11
  648.8 14.9 %collective-permute-start = (bf16[128,3584]{1,0:T(8,128)(2,1)}, bf16[128,3584]{1,0:T(8,128)(2,1)S(1)}, u32[]{:S(2)}, u32[]{:S(2)}) collective-permute-start(bf16[128,3584]{1,0:T(8,128)(2,1)} %get-tuple-element.349), channel_id=1, source_target_pairs={{16,0},{32,16},{48,32},{64,48},{80,64},{96,80},{112,96},{17,1},{33... | collective-permute-start | bytes 2752520 | tf_op jit(solution)/shard_map/while/body/eval_jaxpr/ppermute | solution.py:11
  682.7 14.9 %collective-permute-start = (bf16[128,3584]{1,0:T(8,128)(2,1)}, bf16[128,3584]{1,0:T(8,128)(2,1)S(1)}, u32[]{:S(2)}, u32[]{:S(2)}) collective-permute-start(bf16[128,3584]{1,0:T(8,128)(2,1)} %get-tuple-element.349), channel_id=1, source_target_pairs={{16,0},{32,16},{48,32},{64,48},{80,64},{96,80},{112,96},{17,1},{33... | collective-permute-start | bytes 2752520 | tf_op jit(solution)/shard_map/while/body/eval_jaxpr/ppermute | solution.py:11
  716.5 4.6 collective-permute-start
  746.1 15.3 %all-to-all-start.2 = ((f32[16,32,224]{2,1,0:T(8,128)}), f32[16,32,224]{2,1,0:T(8,128)S(1)}, u32[]{:S(2)}, u32[]{:S(2)}) async-start(f32[16,32,224]{2,1,0:T(8,128)} %copy.13), calls=%async_computation.2 | async-start | bytes 1048576 | tf_op jit(solution)/shard_map/all_to_all | solution.py:33
